TPU v7x, 256 devices: a whole 4x4x8 slice. The times are simulated.
256 devices in a mesh: field: 32 (over z, x), vrow: 2 (over core), vcol: 4 (over y).
Axes of the slice: x: 4, y: 4, z: 8, core: 2. Of those that a mesh axis runs over, the one named last changes fastest.
Arguments:
- blocks: bfloat16 [1024, 192, 2, 256], P(('vrow', 'vcol'), 'field'), may hold values from 0 to 1
- block_ids: int32 [8, 32, 6], P(('vrow', 'vcol'), 'field'), may hold values from 0 to 11, as said below
- block_counts: int32 [8, 32], P(('vrow', 'vcol'), 'field'), may hold values from 1 to 6, as said below
Outputs:
- tables: float32 [1024, 2, 2, 4, 2, 128], P(('vrow', 'field'), None, None, 'vcol')
Inputs may be any that keep to these rules, and one draw needn't show every extreme that they name: `block_ids`: within each row of the last dimension the entries are distinct. `block_counts`: 6 is reached in every draw.
All inputs are finite; a program needn't handle non-finite values.
Results may differ from a plain program's by a relative error of at most 0.0003.
Values may be sent and summed in bfloat16 or wider, within the bound.
No kernel may reach another device: no remote copies, remote signals or barrier semaphores. Data moves between devices by JAX's collectives and lax.ppermute only.
A program may use at most 64 MiB of HBM per device.

v0:
```python
import math
import jax
import jax.numpy as jnp
from jax import lax
from jax.sharding import PartitionSpec as P

SBLK = 12
BLOCK = 256


def side_by_side(arrays, axis, dim, along):
    widths = [math.prod(a.shape[along:]) for a in arrays]
    both = jnp.concatenate(
        [a.reshape(*a.shape[:along], w) for a, w in zip(arrays, widths)], axis=along
    )
    out = lax.all_gather(both, axis, axis=dim, tiled=True)
    parts = jnp.split(out, [sum(widths[:k]) for k in range(1, len(widths))], axis=along)
    return tuple((b.reshape(*out.shape[:along], *a.shape[along:]) for a, b in zip(arrays, parts)))


def split_up(array, dim, length):
    dims = array.shape
    parts = array.reshape(*dims[:dim], length, dims[dim] // length, *dims[dim + 1 :])
    return jnp.moveaxis(parts, dim, 0)


def sent_and_summed(array, axis, dim):
    length = lax.axis_size(axis)
    parts = lax.all_to_all(split_up(array, dim, length), axis, 0, 0, tiled=True)
    return jnp.sum(parts, axis=0)


def expand(blocks, block_ids, block_counts):
    shards = block_ids.shape[0]
    occ = block_ids.shape[-1]
    shaped = blocks.reshape(shards, blocks.shape[0] // shards, occ, 2, blocks.shape[-1])
    slots = jnp.arange(occ, dtype=jnp.int32)
    live = slots[None, :] < block_counts[:, 0][:, None]
    onehot = (block_ids[:, 0, :, None] == jnp.arange(SBLK, dtype=jnp.int32)[None, None, :]) & live[
        ..., None
    ]
    dense = jnp.einsum(
        "sok,svocx->svkcx", onehot.astype(jnp.bfloat16), shaped, preferred_element_type=jnp.float32
    )
    return dense.astype(jnp.bfloat16).reshape(blocks.shape[0], SBLK, 2, blocks.shape[-1])


def on_device(blocks, block_ids, block_counts):
    row_data, row_ids, row_counts = (
        lax.all_gather(blocks, "vcol", axis=0, tiled=True),
        *side_by_side((block_ids, block_counts), "vcol", 0, 2),
    )
    rows = expand(row_data, row_ids, row_counts)
    col_data, col_ids, col_counts = (
        lax.all_gather(blocks, "vrow", axis=0, tiled=True),
        *side_by_side((block_ids, block_counts), "vrow", 0, 2),
    )
    columns = expand(col_data, col_ids, col_counts)
    groups = lax.axis_size("vrow")
    columns = columns.reshape(groups, columns.shape[0] // groups, SBLK, 2, columns.shape[-1])
    fields = lax.axis_size("field")
    term = jnp.einsum("ikcx,rjkdx->icrdj", rows, columns, preferred_element_type=jnp.float32)
    summed = sent_and_summed(term[:, :, :, None], "field", 0)
    return summed / (fields * SBLK * BLOCK)


def solution(mesh):
    placed = (
        P(("vrow", "vcol"), "field", None, None),
        P(("vrow", "vcol"), "field", None),
        P(("vrow", "vcol"), "field"),
    )
    return jax.shard_map(
        on_device,
        mesh=mesh,
        in_specs=placed,
        out_specs=P(("vrow", "field"), None, None, "vcol", None, None),
        check_vma=False,
    )
```

profile of v0, /device:TPU:2, one launch (start us, length us, event | category | flops | bytes accessed | tf_op | source)
XLA Modules:
  0.0 164.3 jit_solution(4973293619530026705)
XLA Ops:
  6.5 0.0 all-gather.3.cloned.1.call-start
  6.5 0.7 all-gather.3.cloned.1.call-update
  7.3 0.0 all-gather.5.cloned.1.call-start
  7.3 0.7 all-gather.5.cloned.1.call-update
  8.7 0.7 pad_add_fusion
  9.4 1.8 %all_gather.12 = s32[2,1,7]{2,1,0:T(1,128)S(1)} all-gather(s32[1,1,7]{2,1,0:T(1,128)S(1)} %pad_add_fusion), channel_id=1, replica_groups=mesh['field'=32,'vrow'=2,'vcol'=4] {'vrow'}, dimensions={0}, use_global_device_ids=true | all-gather | bytes 84 | tf_op jit(solution)/shard_map/all_gather | solution.py:16
  11.2 10.0 %all_gather.14 = s32[4,1,7]{2,1,0:T(1,128)S(1)} all-gather(s32[1,1,7]{2,1,0:T(1,128)S(1)} %pad_add_fusion), channel_id=1, replica_groups=mesh['field'=32,'vrow'=2,'vcol'=4] {'vcol'}, dimensions={0}, use_global_device_ids=true | all-gather | bytes 140 | tf_op jit(solution)/shard_map/all_gather | solution.py:16
  21.1 0.2 slice_reduce_fusion.1
  21.3 0.2 slice_reduce_fusion
  21.6 0.1 iota_compare_fusion.2
  21.6 0.1 iota_compare_fusion.3
  21.7 5.5 %all-gather.3.cloned.1.call-done = bf16[256,6,2,256]{3,2,1,0:T(2,128)(2,1)} async-done(((bf16[128,6,2,256]{3,2,1,0:T(2,128)(2,1)}), bf16[256,6,2,256]{3,2,1,0:T(2,128)(2,1)}) %all-gather.3.cloned.1.call-update) | async-done | bytes 1572880 | tf_op jit(solution)/shard_map/all_gather | solution.py:55
  27.2 1.9 %copy.9 = bf16[256,6,2,256]{3,1,2,0:T(8,128)(2,1)S(1)} copy(bf16[256,6,2,256]{3,2,1,0:T(2,128)(2,1)} %all-gather.3.cloned.1.call-done) | data formatting | bytes 3145728 | tf_op jit(solution)/shard_map/all_gather | solution.py:55
  29.1 3.1 %convert_bitcast_fusion = bf16[2,128,12,2,256,1]{4,2,3,1,0,5:T(8,128)(2,1)} fusion(bf16[2,128,6,2,256]{4,2,3,1,0:T(8,128)(2,1)S(1)} %bitcast.39, s32[2,6]{1,0:T(2,128)S(1)} %bitcast.42, pred[2,6]{1,0:T(4,128)(4,1)S(1)} %iota_compare_fusion.3), kind=kOutput, calls=%fused_computation.3 | convolution fusion | flops 20447520 | bytes 4718652 | tf_op jit(solution)/shard_map/sok,svocx->svkcx/dot_general | solution.py:42
  32.2 40.3 %all-gather.5.cloned.1.call-done = bf16[512,6,2,256]{3,2,1,0:T(2,128)(2,1)} async-done(((bf16[128,6,2,256]{3,2,1,0:T(2,128)(2,1)}), bf16[512,6,2,256]{3,2,1,0:T(2,128)(2,1)}) %all-gather.5.cloned.1.call-update) | async-done | bytes 3145744 | tf_op jit(solution)/shard_map/all_gather | solution.py:50
  72.4 2.9 %copy.10 = bf16[512,6,2,256]{3,1,2,0:T(8,128)(2,1)S(1)} copy(bf16[512,6,2,256]{3,2,1,0:T(2,128)(2,1)} %all-gather.5.cloned.1.call-done) | data formatting | bytes 6291456 | tf_op jit(solution)/shard_map/all_gather | solution.py:50
  75.3 0.0 copy-start
  75.3 4.4 %convolution_convert_fusion = bf16[4,12,128,2,256]{4,1,3,2,0:T(8,128)(2,1)S(1)} fusion(bf16[4,128,6,2,256]{4,2,3,1,0:T(8,128)(2,1)S(1)} %bitcast.37, s32[4,6]{1,0:T(4,128)S(1)} %bitcast.41, pred[4,6]{1,0:T(4,128)(4,1)S(1)} %iota_compare_fusion.2), kind=kOutput, calls=%fused_computation | convolution fusion | flops 40895040 | bytes 9437304 | tf_op jit(solution)/shard_map/sok,svocx->svkcx/dot_general | solution.py:42
  79.8 0.0 copy-done
  79.8 14.4 %fusion.3 = f32[512,2,2,2,128]{0,4,1,3,2:T(8,128)} fusion(bf16[512,12,2,256,1,1]{3,1,2,0,5,4:T(8,128)(2,1)S(1)} %bitcast.38, bf16[2,128,12,2,256,1]{4,2,3,1,0,5:T(8,128)(2,1)S(1)} %copy-done), kind=kOutput, calls=%fused_computation.5 | convolution fusion | flops 3221225472 | bytes 11534336 | tf_op jit(solution)/shard_map/ikcx,rjkdx->icrdj/dot_general | solution.py:62
  94.2 1.9 %copy.13 = f32[512,2,2,2,128]{4,0,3,2,1:T(8,128)S(1)} copy(f32[512,2,2,2,128]{0,4,1,3,2:T(8,128)} %fusion.3) | data formatting | bytes 4194304 | tf_op jit(solution)/shard_map/ikcx,rjkdx->icrdj/transpose | solution.py:62
  96.1 0.3 copy.14
  96.3 60.3 %all_to_all.5 = f32[32,16,2,2,1,2,128]{6,1,5,3,2,4,0:T(8,128)S(1)} all-to-all(f32[32,16,2,2,1,2,128]{6,1,5,3,2,4,0:T(8,128)S(1)} %copy.14), channel_id=1, replica_groups=mesh['field'=32,'vrow'=2,'vcol'=4] {'field'}, dimensions={0} | all-to-all | bytes 4194304 | tf_op jit(solution)/shard_map/all_to_all | solution.py:29
  156.6 0.1 reduce_sum.9
  156.8 0.7 copy.16
  (1 shorter events, 0.0 us)
Async XLA Ops:
  6.5 20.7 %all-gather.3.cloned.1.call-start = ((), (), s32[]{:S(2)}) async-start(), calls=%async_computation.1 | async-start | bytes 2359296 | tf_op jit(solution)/shard_map/all_gather | solution.py:55
  7.3 65.2 %all-gather.5.cloned.1.call-start = ((), (), s32[]{:S(2)}) async-start(), calls=%async_computation.2 | async-start | bytes 3932160 | tf_op jit(solution)/shard_map/all_gather | solution.py:50
  75.3 4.5 %copy-start = (bf16[2,128,12,2,256,1]{4,2,3,1,0,5:T(8,128)(2,1)S(1)}, bf16[2,128,12,2,256,1]{4,2,3,1,0,5:T(8,128)(2,1)}, u32[]{:S(2)}) copy-start(bf16[2,128,12,2,256,1]{4,2,3,1,0,5:T(8,128)(2,1)} %convert_bitcast_fusion) | copy-start | bytes 9437188
Sparse Core Ops, SparseCore 0:
  9.1 18.0 all-gather.2
  29.1 43.3 all-gather.4
where the time goes:
time: 165 us; the launch traced here: 164 us
  blocking collectives  72.1 us (44%)
  waiting for transfers between devices  47.2 us (29%)
  matrix products  21.9 us (13%)
  between operations  14.1 us (9%)
  local copies, waits for them, and re-layouts  7.99 us (5%)
    all_to_all x1, blocking collectives, sent_and_summed(): parts = lax.all_to_all(split_up(array, dim, length), axis, 0, 0, tiled=True)  60.3 us
    all_gather x1, waiting for transfers between devices, on_device(): lax.all_gather(blocks, 'vcol', axis=0, tiled=True)  40.3 us
    dot_general x1, matrix products, on_device(): jnp.einsum('ikcx,rjkdx->icrdj', rows, columns, preferred_element_type=jnp...  14.4 us
    all_gather x2, blocking collectives, side_by_side(): out = lax.all_gather(both, axis, axis=dim, tiled=True)  11.8 us
    dot_general x2, matrix products, expand(): jnp.einsum('sok,svocx->svkcx', onehot.astype(jnp.bfloat16), shaped, prefe...  7.51 us
    all_gather x1, waiting for transfers between devices, on_device(): lax.all_gather(blocks, 'vrow', axis=0, tiled=True)  5.53 us
  transfers between devices with their start and end apart: 2, of which 2 were waited for; matrix products, arithmetic and copies ran while one was open for 4% of the time, Pallas kernels for 0%

commit v1 on v0

--- a/solution.py
+++ b/solution.py
@@ -3,9 +3,18 @@
 import jax.numpy as jnp
 from jax import lax
 from jax.sharding import PartitionSpec as P
+from jax.lax import all_to_all, axis_size
 
 SBLK = 12
 BLOCK = 256
+
+
+def load_the_lane(work_x):
+    group_axis = "vcol"
+    n_dev_all = axis_size(group_axis)
+    line_up = list(map(lambda rr: n_dev_all if rr == 0 else 1, range(work_x.ndim)))
+    y2 = all_to_all(jnp.tile(work_x, line_up), group_axis, split_axis=0, concat_axis=0, tiled=True)
+    return y2
 
 
 def side_by_side(arrays, axis, dim, along):
@@ -47,7 +56,7 @@
 
 def on_device(blocks, block_ids, block_counts):
     row_data, row_ids, row_counts = (
-        lax.all_gather(blocks, "vcol", axis=0, tiled=True),
+        load_the_lane(blocks),
         *side_by_side((block_ids, block_counts), "vcol", 0, 2),
     )
     rows = expand(row_data, row_ids, row_counts)

time: 165 us -> 151 us (0.915)
  waiting for transfers between devices: 47.2 us -> 0.71 us
  blocking collectives: 72.1 us -> 98.3 us
  starting transfers between devices: 0.04 us -> 4.6 us
  local copies, waits for them, and re-layouts: 7.99 us -> 10.5 us
    all_gather x1 -> x0, waiting for transfers between devices: 40.3 us -> none  [on_device(): lax.all_gather(blocks, 'vcol', axis=0, tiled=True)]
    all_gather x2, blocking collectives: 11.8 us -> 38.2 us  [side_by_side(): out = lax.all_gather(both, axis, axis=dim, tiled=True)]
    all_gather x1, waiting for transfers between devices: 5.53 us -> 0.01 us  [on_device(): lax.all_gather(blocks, 'vrow', axis=0, tiled=True)]
    all_to_all x0 -> x1, starting transfers between devices: none -> 4.59 us  [load_the_lane(): all_to_all(jnp.tile(work_x, line_up), group_axis, split_axis=0, concat_ax...]
    another operation x0 -> x1, local copies, waits for them, and re-layouts: none -> 4.43 us  [load_the_lane(): jnp.tile(work_x, line_up)]
    all_gather x1 -> x0, local copies, waits for them, and re-layouts: 2.87 us -> none  [on_device(): lax.all_gather(blocks, 'vcol', axis=0, tiled=True)]
  transfers between devices with their start and end apart: 2 -> 2, of which waited for: 2 -> 0; matrix products, arithmetic and copies ran while one was open for 4% -> 4% of each run, Pallas kernels for 0% -> 0%
where the time goes in v1:
time: 151 us
  blocking collectives  98.3 us (65%)
  matrix products  21.9 us (15%)
  between operations  14.1 us (9%)
  local copies, waits for them, and re-layouts  10.5 us (7%)
  starting transfers between devices  4.6 us (3%)
    all_to_all x1, blocking collectives, sent_and_summed(): parts = lax.all_to_all(split_up(array, dim, length), axis, 0, 0, tiled=True)  60.1 us
    all_gather x2, blocking collectives, side_by_side(): out = lax.all_gather(both, axis, axis=dim, tiled=True)  38.2 us
    dot_general x1, matrix products, on_device(): jnp.einsum('ikcx,rjkdx->icrdj', rows, columns, preferred_element_type=jnp...  14.4 us
    dot_general x2, matrix products, expand(): jnp.einsum('sok,svocx->svkcx', onehot.astype(jnp.bfloat16), shaped, prefe...  7.5 us
    all_to_all x1, starting transfers between devices, load_the_lane(): all_to_all(jnp.tile(work_x, line_up), group_axis, split_axis=0, concat_ax...  4.59 us
    another operation x1, local copies, waits for them, and re-layouts, load_the_lane(): jnp.tile(work_x, line_up)  4.43 us
  transfers between devices with their start and end apart: 2, of which 0 were waited for; matrix products, arithmetic and copies ran while one was open for 4% of the time, Pallas kernels for 0%

profile of v1, /device:TPU:2, one launch (start us, length us, event | category | flops | bytes accessed | tf_op | source)
XLA Modules:
  0.0 150.6 jit_solution(12868515497530148212)
XLA Ops:
  6.5 4.4 %tile.4 = bf16[4,128,6,2,256]{4,3,2,1,0:T(2,128)(2,1)} broadcast(bf16[128,6,2,256]{3,2,1,0:T(2,128)(2,1)} %param.3), dimensions={1,2,3,4} | broadcast | bytes 3932160 | tf_op jit(solution)/shard_map/tile | solution.py:16
  11.0 0.0 copy-start.1
  11.0 4.6 %all-to-all-start = ((bf16[512,6,2,256]{3,2,1,0:T(2,128)(2,1)}), bf16[512,6,2,256]{3,2,1,0:T(2,128)(2,1)S(1)}, u32[]{:S(2)}, u32[]{:S(2)}) async-start(bf16[512,6,2,256]{3,2,1,0:T(2,128)(2,1)} %bitcast.39), calls=%async_computation | async-start | bytes 6291456 | tf_op jit(solution)/shard_map/all_to_all | solution.py:16
  15.6 0.0 all-gather.2.cloned.1.call-start
  15.6 0.7 all-gather.2.cloned.1.call-update
  16.9 0.0 copy-done.1
  16.9 0.1 pad_add_fusion
  17.0 1.8 %all_gather.9 = s32[2,1,7]{2,1,0:T(1,128)S(1)} all-gather(s32[1,1,7]{2,1,0:T(1,128)S(1)} %pad_add_fusion), channel_id=1, replica_groups=mesh['field'=32,'vrow'=2,'vcol'=4] {'vrow'}, dimensions={0}, use_global_device_ids=true | all-gather | bytes 84 | tf_op jit(solution)/shard_map/all_gather | solution.py:25
  18.8 36.4 %all_gather.11 = s32[4,1,7]{2,1,0:T(1,128)S(1)} all-gather(s32[1,1,7]{2,1,0:T(1,128)S(1)} %pad_add_fusion), channel_id=1, replica_groups=mesh['field'=32,'vrow'=2,'vcol'=4] {'vcol'}, dimensions={0}, use_global_device_ids=true | all-gather | bytes 140 | tf_op jit(solution)/shard_map/all_gather | solution.py:25
  55.2 0.2 slice_reduce_fusion.1
  55.4 0.2 slice_reduce_fusion
  55.7 0.1 iota_compare_fusion.2
  55.8 0.1 iota_compare_fusion.3
  55.8 0.0 all-gather.2.cloned.1.call-done
  55.8 1.9 %copy.9 = bf16[256,6,2,256]{3,1,2,0:T(8,128)(2,1)S(1)} copy(bf16[256,6,2,256]{3,2,1,0:T(2,128)(2,1)} %all-gather.2.cloned.1.call-done) | data formatting | bytes 3145728 | tf_op jit(solution)/shard_map/all_gather | solution.py:64
  57.7 3.1 %convert_bitcast_fusion = bf16[2,128,12,2,256,1]{4,2,3,1,0,5:T(8,128)(2,1)} fusion(bf16[2,128,6,2,256]{4,2,3,1,0:T(8,128)(2,1)S(1)} %bitcast.41, s32[2,6]{1,0:T(2,128)S(1)} %bitcast.44, pred[2,6]{1,0:T(4,128)(4,1)S(1)} %iota_compare_fusion.3), kind=kOutput, calls=%fused_computation.3 | convolution fusion | flops 20447520 | bytes 4718652 | tf_op jit(solution)/shard_map/sok,svocx->svkcx/dot_general | solution.py:51
  60.8 0.0 all-to-all-done
  60.8 1.0 copy.10
  61.8 0.0 copy-start
  61.8 4.4 %convolution_convert_fusion = bf16[4,12,128,2,256]{4,1,3,2,0:T(8,128)(2,1)S(1)} fusion(bf16[4,128,6,2,256]{4,2,3,1,0:T(8,128)(2,1)S(1)} %bitcast.38, s32[4,6]{1,0:T(4,128)S(1)} %bitcast.43, pred[4,6]{1,0:T(4,128)(4,1)S(1)} %iota_compare_fusion.2), kind=kOutput, calls=%fused_computation | convolution fusion | flops 40895040 | bytes 9437304 | tf_op jit(solution)/shard_map/sok,svocx->svkcx/dot_general | solution.py:51
  66.2 0.0 copy-done
  66.2 14.4 %fusion.3 = f32[512,2,2,2,128]{0,4,1,3,2:T(8,128)} fusion(bf16[512,12,2,256,1,1]{3,1,2,0,5,4:T(8,128)(2,1)S(1)} %bitcast.40, bf16[2,128,12,2,256,1]{4,2,3,1,0,5:T(8,128)(2,1)S(1)} %copy-done), kind=kOutput, calls=%fused_computation.5 | convolution fusion | flops 3221225472 | bytes 11534336 | tf_op jit(solution)/shard_map/ikcx,rjkdx->icrdj/dot_general | solution.py:71
  80.6 1.9 %copy.13 = f32[512,2,2,2,128]{4,0,3,2,1:T(8,128)S(1)} copy(f32[512,2,2,2,128]{0,4,1,3,2:T(8,128)} %fusion.3) | data formatting | bytes 4194304 | tf_op jit(solution)/shard_map/ikcx,rjkdx->icrdj/transpose | solution.py:71
  82.5 0.3 copy.14
  82.8 60.1 %all_to_all.10 = f32[32,16,2,2,1,2,128]{6,1,5,3,2,4,0:T(8,128)S(1)} all-to-all(f32[32,16,2,2,1,2,128]{6,1,5,3,2,4,0:T(8,128)S(1)} %copy.14), channel_id=1, replica_groups=mesh['field'=32,'vrow'=2,'vcol'=4] {'field'}, dimensions={0} | all-to-all | bytes 4194304 | tf_op jit(solution)/shard_map/all_to_all | solution.py:38
  142.9 0.1 reduce_sum.9
  143.1 0.7 copy.16
  (1 shorter events, 0.0 us)
Async XLA Ops:
  11.0 6.0 %copy-start.1 = (s32[1,1,6]{2,1,0:T(1,128)S(1)}, s32[1,1,6]{2,1,0:T(1,128)}, u32[]{:S(2)}) copy-start(s32[1,1,6]{2,1,0:T(1,128)} %param.4) | copy-start | bytes 76
  11.0 49.8 %all-to-all-start = ((bf16[512,6,2,256]{3,2,1,0:T(2,128)(2,1)}), bf16[512,6,2,256]{3,2,1,0:T(2,128)(2,1)S(1)}, u32[]{:S(2)}, u32[]{:S(2)}) async-start(bf16[512,6,2,256]{3,2,1,0:T(2,128)(2,1)} %bitcast.39), calls=%async_computation | async-start | bytes 6291456 | tf_op jit(solution)/shard_map/all_to_all | solution.py:16
  15.6 40.3 %all-gather.2.cloned.1.call-start = ((), (), s32[]{:S(2)}) async-start(), calls=%async_computation.2 | async-start | bytes 2359296 | tf_op jit(solution)/shard_map/all_gather | solution.py:64
  61.8 4.5 %copy-start = (bf16[2,128,12,2,256,1]{4,2,3,1,0,5:T(8,128)(2,1)S(1)}, bf16[2,128,12,2,256,1]{4,2,3,1,0,5:T(8,128)(2,1)}, u32[]{:S(2)}) copy-start(bf16[2,128,12,2,256,1]{4,2,3,1,0,5:T(8,128)(2,1)} %convert_bitcast_fusion) | copy-start | bytes 9437188
Sparse Core Ops, SparseCore 0:
  18.2 18.4 all-gather.1
